TPU v7x, 128 devices: a whole 4x4x4 slice. The times are simulated.
128 devices in a mesh: walk: 8 (over y, z_hi), chol: 16 (over z_lo, x, core).
Axes of the slice: x: 4, y: 4, z: 4 (z_hi: 2, z_lo: 2; z = z_hi * 2 + z_lo), core: 2. Of those that a mesh axis runs over, the one named last changes fastest.
Arguments:
- orbitals: bfloat16 [1024, 64, 1024], P(('walk', 'chol')), may hold values from -6 to 6
- cholesky: bfloat16 [192, 64, 1024], P('chol'), may hold values from -0.1875 to 0.1875
- parents: int32 [1024], P(('walk', 'chol')), may hold values from 0 to 1023, as said below
- counts: int32 [8, 16], P('walk', 'chol'), may hold values from 1 to 8, as said below
- steps: bfloat16 [1024, 64, 1024], P(('walk', 'chol')), may hold values from -6 to 6
Outputs:
- energy: float32 [1024], P(('walk', 'chol'))
- parent_grad: float32 [1024, 64, 1024], P(('walk', 'chol'))
Inputs may be any that keep to these rules, and one draw needn't show every extreme that they name: The parent of a new walker lies on the same index of chol as the walker. Of one device's new walkers at most 2 have parents on any one index of walk, and on some index exactly 2. The first counts entries of a device's 8 new walkers are live; in every draw some device is full.
All inputs are finite; a program needn't handle non-finite values.
Results may differ from a plain program's by a relative error of at most 0.0044.
Values may be sent and summed in bfloat16 or wider, within the bound.
A program may use at most 128 MiB of HBM per device.

v0:
```python
import jax
import jax.numpy as jnp
from jax import lax
from jax.sharding import Mesh
from jax.sharding import PartitionSpec as P

CAP = 2
WALK = ("walk_0", "walk_1")
WALK_CHOL = ("walk_0", "walk_1", "chol")


def cut_along(shard, dim, devices):
    before, after = (shard.shape[:dim], shard.shape[dim + 1 :])
    return jnp.moveaxis(shard.reshape(*before, devices, -1, *after), dim, 0)


def in_order(parts, dim):
    shape = list(parts.shape[1:])
    shape[dim] *= parts.shape[0]
    return jnp.moveaxis(parts, 0, dim).reshape(shape)


def turned_blocks(parts, axes, sequence):
    shape = [lax.axis_size(a) for a in axes]
    parts = parts.reshape(*shape, *parts.shape[1:])
    for k in sequence:
        parts = lax.all_to_all(parts, axes[k], split_axis=k, concat_axis=k, tiled=True)
    return parts.reshape(-1, *parts.shape[len(axes) :])


def one_axis_at_a_time(shard, axes, sequence, split_dim, concat_dim):
    parts = cut_along(shard, split_dim, lax.axis_size(axes))
    return in_order(turned_blocks(parts, axes, sequence), concat_dim)


def body(orbitals, cholesky, parents, counts, steps):
    walk_size = lax.axis_size(WALK)
    chol_size = lax.axis_size("chol")
    per_device = orbitals.shape[0]
    electrons = orbitals.shape[1]
    basis_len = orbitals.shape[2]
    vectors_dev = cholesky.shape[0]
    source_walk = parents // (chol_size * per_device)
    source_slot = parents % per_device
    position = jnp.arange(per_device, dtype=jnp.int32)
    earlier_same = (source_walk[:, None] == source_walk[None, :]) & (
        position[None, :] < position[:, None]
    )
    rank_within = jnp.sum(earlier_same.astype(jnp.int32), axis=1)
    slot_ids = source_walk * CAP + rank_within
    flat_slots = jnp.arange(walk_size * CAP, dtype=jnp.int32)
    matching = slot_ids[:, None] == flat_slots[None, :]
    wanted = jnp.sum(matching.astype(jnp.int32) * (source_slot[:, None] + 1), axis=0) - 1
    asked = one_axis_at_a_time(wanted.reshape(walk_size, CAP), WALK, (0, 1), 0, 0).reshape(-1)
    picker = (asked[:, None] == position[None, :]).astype(jnp.bfloat16)
    outgoing = jnp.dot(picker, orbitals.reshape(per_device, -1), preferred_element_type=jnp.float32)
    outgoing = outgoing.astype(jnp.bfloat16).reshape(walk_size, CAP, electrons, basis_len)
    incoming = lax.all_to_all(outgoing, WALK, split_axis=0, concat_axis=0, tiled=True)
    gathered = jnp.dot(
        matching.astype(jnp.bfloat16),
        incoming.reshape(walk_size * CAP, -1),
        preferred_element_type=jnp.float32,
    )
    clones = gathered + steps.reshape(per_device, -1).astype(jnp.float32)
    clones = clones.astype(jnp.bfloat16).reshape(per_device, electrons, basis_len)
    piece = lax.all_gather(cholesky, "chol", axis=0, tiled=True)
    shards = piece.shape[0] // vectors_dev
    blocks = piece.reshape(shards, vectors_dev, electrons, basis_len)
    intersection = jnp.einsum(
        "sgip,wjp->swgij", blocks, clones, preferred_element_type=jnp.float32
    ).astype(jnp.bfloat16)
    part = -jnp.einsum("swgji,sgip->swjp", intersection, blocks, preferred_element_type=jnp.float32)
    part = lax.optimization_barrier(part.astype(jnp.bfloat16))
    gradient = jnp.sum(part.astype(jnp.float32), axis=0)
    alive = (position < counts.reshape(-1)[0]).astype(jnp.float32)
    gradient = gradient * alive[:, None, None]
    energy = 0.5 * jnp.sum(clones.astype(jnp.float32) * gradient, axis=(1, 2))
    backward = jnp.dot(
        matching.T.astype(jnp.float32),
        gradient.reshape(per_device, -1),
        precision=lax.Precision.HIGHEST,
    )
    backward = backward.reshape(walk_size, CAP, electrons, basis_len)
    returned = lax.all_to_all(backward, WALK, split_axis=0, concat_axis=0, tiled=True)
    owner = (asked[None, :] == position[:, None]).astype(jnp.float32)
    parent_grad = jnp.dot(
        owner, returned.reshape(walk_size * CAP, -1), precision=lax.Precision.HIGHEST
    )
    return (energy, parent_grad.reshape(per_device, electrons, basis_len))


def solution(mesh):
    torus = Mesh(mesh.devices.reshape(4, 2, mesh.shape["chol"]), ("walk_0", "walk_1", "chol"))
    return jax.shard_map(
        body,
        mesh=torus,
        in_specs=(
            P(WALK_CHOL, None, None),
            P("chol", None, None),
            P(WALK_CHOL),
            P(WALK, "chol"),
            P(WALK_CHOL, None, None),
        ),
        out_specs=(P(WALK_CHOL), P(WALK_CHOL, None, None)),
        check_vma=False,
    )
```

profile of v0, /device:TPU:1, one launch (start us, length us, event | category | flops | bytes accessed | tf_op | source)
XLA Modules:
  0.0 311.1 jit_solution(2648531284516923733)
XLA Ops:
  7.2 0.0 copy-start.2
  7.2 0.0 all-gather.2.cloned.1.call-start
  7.2 0.7 all-gather.2.cloned.1.call-update
  7.9 0.7 and_select_fusion.1
  8.6 0.2 convert_reduce_fusion.1
  8.8 0.1 select_reduce_fusion
  8.9 0.7 sub.11
  9.5 5.0 %all-to-all-start = ((s32[4,2,1,2]{3,1,2,0:T(2,128)}), s32[4,2,1,2]{3,1,2,0:T(2,128)S(1)}, u32[]{:S(2)}, u32[]{:S(2)}) async-start(s32[4,2,1,2]{3,1,2,0:T(2,128)} %bitcast), calls=%async_computation | async-start | bytes 8192 | tf_op jit(solution)/shard_map/all_to_all | solution.py:27
  14.5 0.0 copy-done.2
  14.6 0.6 copy.35
  15.1 3.6 %all-to-all-done = s32[4,2,1,2]{3,1,2,0:T(2,128)S(1)} async-done(((s32[4,2,1,2]{3,1,2,0:T(2,128)}), s32[4,2,1,2]{3,1,2,0:T(2,128)S(1)}, u32[]{:S(2)}, u32[]{:S(2)}) %all-to-all-start) | async-done | bytes 96 | tf_op jit(solution)/shard_map/all_to_all | solution.py:27
  18.7 0.1 copy.20
  18.8 8.9 %all_to_all.20 = s32[4,2,1,2]{0,3,2,1:T(2,128)S(1)} all-to-all(s32[4,2,1,2]{0,3,2,1:T(2,128)S(1)} %copy.20), channel_id=1, replica_groups=mesh['walk_0'=4,'walk_1'=2,'chol'=16] {'walk_1'}, dimensions={1} | all-to-all | bytes 128 | tf_op jit(solution)/shard_map/all_to_all | solution.py:27
  27.7 0.1 copy.21
  27.8 0.1 eq.84
  27.9 0.8 convolution_convert_fusion
  28.7 2.5 copy.36
  31.2 0.0 copy-start.1
  31.2 3.7 %all-to-all-start.2 = ((bf16[8,2,64,1024]{3,2,1,0:T(8,128)(2,1)}), bf16[8,2,64,1024]{3,2,1,0:T(8,128)(2,1)S(1)}, u32[]{:S(2)}, u32[]{:S(2)}) async-start(bf16[8,2,64,1024]{3,2,1,0:T(8,128)(2,1)} %bitcast.74), calls=%async_computation.2 | async-start | bytes 4194304 | tf_op jit(solution)/shard_map/all_to_all | solution.py:58
  34.9 0.0 copy-done.1
  35.0 0.2 convert_bitcast_fusion
  35.2 2.5 copy.38
  38.4 28.2 %all-to-all-done.2 = bf16[8,2,64,1024]{3,2,1,0:T(8,128)(2,1)S(1)} async-done(((bf16[8,2,64,1024]{3,2,1,0:T(8,128)(2,1)}), bf16[8,2,64,1024]{3,2,1,0:T(8,128)(2,1)S(1)}, u32[]{:S(2)}, u32[]{:S(2)}) %all-to-all-start.2) | async-done | bytes 2097184 | tf_op jit(solution)/shard_map/all_to_all | solution.py:58
  66.7 0.0 copy-start
  66.7 1.2 copy.37
  67.8 0.4 copy-done
  68.3 0.5 fusion
  68.8 98.2 %all-gather.2.cloned.1.call-done = bf16[192,64,1024]{2,1,0:T(8,128)(2,1)} async-done(((bf16[12,64,1024]{2,1,0:T(8,128)(2,1)}), bf16[192,64,1024]{2,1,0:T(8,128)(2,1)}) %all-gather.2.cloned.1.call-update) | async-done | bytes 25165840 | tf_op jit(solution)/shard_map/all_gather | solution.py:66
  166.9 47.7 %fusion.1 = bf16[16,8,64,1024]{3,2,1,0:T(8,128)(2,1)} fusion(bf16[16,12,64,1024,1]{3,2,1,4,0:T(8,128)(2,1)} %bitcast.83, bf16[8,64,1024,1,1]{2,0,1,4,3:T(8,128)(2,1)S(1)} %bitcast.81), kind=kOutput, calls=%fused_computation.4 | convolution fusion | flops 25792872448 | bytes 42991616 | tf_op jit(solution)/shard_map/swgji,sgip->swjp/dot_general | solution.py:72
  214.6 7.3 %convert_reduce_fusion = f32[8,64,1024]{2,1,0:T(8,128)S(1)} fusion(bf16[16,8,64,1024]{3,2,1,0:T(8,128)(2,1)} %fusion.1), kind=kLoop, calls=%fused_computation.5 | loop fusion | flops 16252928 | bytes 18874368 | tf_op jit(solution)/shard_map/reduce_sum | solution.py:74
  222.0 1.2 copy.39
  223.2 0.9 multiply_reduce_fusion
  224.1 1.8 fusion.14
  226.0 4.4 %copy.24 = f32[8,2,64,1024]{3,2,1,0:T(8,128)} copy(f32[8,2,64,1024]{3,0,2,1:T(8,128)S(1)} %fusion.14) | data formatting | bytes 8388608 | tf_op jit(solution)/shard_map/dot_general | solution.py:78
  230.4 6.3 %all-to-all-start.3 = ((f32[8,2,64,1024]{3,2,1,0:T(8,128)}), f32[8,2,64,1024]{3,2,1,0:T(8,128)}, u32[]{:S(2)}, u32[]{:S(2)}) async-start(f32[8,2,64,1024]{3,2,1,0:T(8,128)} %copy.24), calls=%async_computation.3 | async-start | bytes 8388608 | tf_op jit(solution)/shard_map/all_to_all | solution.py:84
  236.6 0.5 broadcast_multiply_fusion.1
  237.1 58.7 %all-to-all-done.3 = f32[8,2,64,1024]{3,2,1,0:T(8,128)} async-done(((f32[8,2,64,1024]{3,2,1,0:T(8,128)}), f32[8,2,64,1024]{3,2,1,0:T(8,128)}, u32[]{:S(2)}, u32[]{:S(2)}) %all-to-all-start.3) | async-done | bytes 4194336 | tf_op jit(solution)/shard_map/all_to_all | solution.py:84
  295.8 5.9 %fusion.9 = f32[8,64,1024]{2,0,1:T(8,128)S(1)} fusion(s32[16]{0:T(128)S(1)} %eq.84, f32[2,8,64,1024]{3,2,1,0:T(8,128)} %bitcast.39), kind=kOutput, calls=%fused_computation.10 | convolution fusion | flops 100663424 | bytes 6291520 | tf_op jit(solution)/shard_map/dot_general | solution.py:86
  301.7 2.5 copy.26
  (4 shorter events, 0.0 us)
Async XLA Ops:
  7.2 7.4 %copy-start.2 = (bf16[8,64,1024]{2,1,0:T(8,128)(2,1)S(1)}, bf16[8,64,1024]{2,1,0:T(8,128)(2,1)}, u32[]{:S(2)}) copy-start(bf16[8,64,1024]{2,1,0:T(8,128)(2,1)} %param.5) | copy-start | bytes 3145732
  7.2 159.8 %all-gather.2.cloned.1.call-start = ((), (), s32[]{:S(2)}) async-start(), calls=%async_computation.4 | async-start | bytes 26738688 | tf_op jit(solution)/shard_map/all_gather | solution.py:66
  9.5 9.1 %all-to-all-start = ((s32[4,2,1,2]{3,1,2,0:T(2,128)}), s32[4,2,1,2]{3,1,2,0:T(2,128)S(1)}, u32[]{:S(2)}, u32[]{:S(2)}) async-start(s32[4,2,1,2]{3,1,2,0:T(2,128)} %bitcast), calls=%async_computation | async-start | bytes 8192 | tf_op jit(solution)/shard_map/all_to_all | solution.py:27
  31.2 3.8 %copy-start.1 = (bf16[8,64,1024]{2,1,0:T(8,128)(2,1)S(1)}, bf16[8,64,1024]{2,1,0:T(8,128)(2,1)}, u32[]{:S(2)}) copy-start(bf16[8,64,1024]{2,1,0:T(8,128)(2,1)} %param.9) | copy-start | bytes 3145732
  31.2 35.5 %all-to-all-start.2 = ((bf16[8,2,64,1024]{3,2,1,0:T(8,128)(2,1)}), bf16[8,2,64,1024]{3,2,1,0:T(8,128)(2,1)S(1)}, u32[]{:S(2)}, u32[]{:S(2)}) async-start(bf16[8,2,64,1024]{3,2,1,0:T(8,128)(2,1)} %bitcast.74), calls=%async_computation.2 | async-start | bytes 4194304 | tf_op jit(solution)/shard_map/all_to_all | solution.py:58
  66.7 1.6 copy-start
  230.4 65.5 %all-to-all-start.3 = ((f32[8,2,64,1024]{3,2,1,0:T(8,128)}), f32[8,2,64,1024]{3,2,1,0:T(8,128)}, u32[]{:S(2)}, u32[]{:S(2)}) async-start(f32[8,2,64,1024]{3,2,1,0:T(8,128)} %copy.24), calls=%async_computation.3 | async-start | bytes 8388608 | tf_op jit(solution)/shard_map/all_to_all | solution.py:84
Sparse Core Ops, SparseCore 0:
  9.7 157.2 all-gather.1
where the time goes:
time: 312 us; the launch traced here: 311 us
  waiting for transfers between devices  189 us (61%)
  matrix products  56.6 us (18%)
  local copies, waits for them, and re-layouts  16.4 us (5%)
  starting transfers between devices  15 us (5%)
  between operations  14.8 us (5%)
  other arithmetic  9.99 us (3%)
  blocking collectives  8.93 us (3%)
    all_gather x1, waiting for transfers between devices, body(): piece = lax.all_gather(cholesky, 'chol', axis=0, tiled=True)  98.2 us
    all_to_all x1, waiting for transfers between devices, body(): lax.all_to_all(backward, WALK, split_axis=0, concat_axis=0, tiled=True)  58.7 us
    dot_general x1, matrix products, body(): jnp.einsum('swgji,sgip->swjp', intersection, blocks, preferred_element_ty...  47.7 us
    all_to_all x1, waiting for transfers between devices, body(): lax.all_to_all(outgoing, WALK, split_axis=0, concat_axis=0, tiled=True)  28.2 us
    unnamed x12, local copies, waits for them, and re-layouts  11 us
    all_to_all x1, blocking collectives, turned_blocks(): lax.all_to_all(parts, axes[k], split_axis=k, concat_axis=k, tiled=True)  8.93 us
    reduce_sum x1, other arithmetic, body(): gradient = jnp.sum(part.astype(jnp.float32), axis=0)  7.34 us
    all_to_all x1, starting transfers between devices, body(): lax.all_to_all(backward, WALK, split_axis=0, concat_axis=0, tiled=True)  6.27 us
  transfers between devices with their start and end apart: 4, of which 4 were waited for; matrix products, arithmetic and copies ran while one was open for 3% of the time, Pallas kernels for 0%

commit v1 on v0

v1 whole, which is shorter than its diff:
```python
import functools

import jax
import jax.numpy as jnp
from jax import lax
from jax.experimental import pallas as pl
from jax.experimental.pallas import tpu as pltpu
from jax.sharding import Mesh
from jax.sharding import PartitionSpec as P

NAMES = ("y", "h", "l", "x", "k")
MESH = pl.DeviceIdType.MESH
CAP = 2
NY, NH, NX = 4, 2, 4
CHUNKS = 4
EARLY = 4

ORDER = ("H0", "H1", "X00", "X01", "X02", "P0", "X03", "X10", "O0", "X11", "O1", "O3", "O2", "P1", "X12", "X13")
BLOCK = {name: i for i, name in enumerate(ORDER)}


def pair_piece(i, dk):
    return (BLOCK[f"P{i // 2}"], (i % 2) * 2 + dk)


def x_piece(dz, side, i, dk):
    return (BLOCK[f"X{dz}{i}"], side + 2 * dk)


def far_piece(dz, r, dk):
    return (BLOCK[f"O{r}"], dz + 2 * dk)


def piece_id(piece):
    return piece[0] * CHUNKS + piece[1]


class Links:
    def __init__(self, store, send_sem, recv_sem, peers, depth):
        self.store, self.send_sem, self.recv_sem = store, send_sem, recv_sem
        self.peers, self.depth = peers, depth
        self.sends = {}

    def view(self, piece):
        return self.store.at[piece[0], pl.ds(piece[1] * self.depth, self.depth)]

    def send(self, source, piece, peer, key=None):
        copy = pltpu.make_async_remote_copy(
            src_ref=source,
            dst_ref=self.view(piece),
            send_sem=self.send_sem.at[self.sends.setdefault((piece, key or peer), len(self.sends))],
            recv_sem=self.recv_sem.at[piece_id(piece)],
            device_id=self.peers[peer],
            device_id_type=MESH,
        )
        copy.start()

    def forward(self, piece, target, peer, key=None):
        self.send(self.view(piece), target, peer, key)

    def any_copy(self, piece, send_sem, recv_sem):
        here = self.view(piece)
        return pltpu.make_async_remote_copy(
            src_ref=here,
            dst_ref=here,
            send_sem=send_sem,
            recv_sem=recv_sem,
            device_id=self.peers["core"],
            device_id_type=MESH,
        )

    def wait(self, piece):
        self.any_copy(piece, self.send_sem.at[0], self.recv_sem.at[piece_id(piece)]).wait_recv()

    def finish(self):
        for n in range(len(self.sends)):
            self.any_copy((0, 0), self.send_sem.at[n], self.recv_sem.at[0]).wait_send()


def half_step(store, turned, inter, total, t):
    electrons, basis = store.shape[2:]
    early, late = t < EARLY, t < 2 * EARLY
    g = jnp.where(late, jnp.where(early, 0, 1), lax.rem(t, 2))
    b = jnp.where(late, jnp.where(early, t, t - EARLY), t // 2)
    block = store.at[b]
    for n in range(turned.shape[2] // 256):
        for m in range(store.shape[1] // 4):
            vectors = block[4 * m : 4 * m + 4].reshape(4 * electrons, basis)
            made = jnp.dot(vectors, turned[g, :, n * 256 : (n + 1) * 256], preferred_element_type=jnp.float32)
            made = made.astype(jnp.bfloat16)
            for v in range(0, 4, 2):
                for s in range(0, 4, 2):
                    a = made[v * 64 : v * 64 + 64, s * 64 : s * 64 + 128]
                    c = made[v * 64 + 64 : v * 64 + 128, s * 64 : s * 64 + 128]
                    row, col = (4 * n + s) * 64, (4 * m + v) * 64
                    inter[row : row + 64, col : col + 128] = jnp.concatenate([a[:, :64], c[:, :64]], axis=1)
                    inter[row + 64 : row + 128, col : col + 128] = jnp.concatenate([a[:, 64:], c[:, 64:]], axis=1)
    for n in range(basis // 256):
        part = block[:, :, n * 256 : (n + 1) * 256].reshape(-1, 256)
        total[g, :, n * 256 : (n + 1) * 256] += jnp.dot(inter[...], part, preferred_element_type=jnp.float32)


def kernel(
    parents, counts, orbitals_hbm, cholesky_hbm, steps_hbm, energy_ref, grad_ref,
    store, orb, stp, out, slots, tag_out, tags, turned, total, inter, weights, e_out, e_in,
    load_sem, slot_send, slot_recv, tag_send, tag_recv, e_send, e_recv, piece_send, piece_recv,
):
    y, h, l, x, k = (lax.axis_index(name) for name in NAMES)
    per_device, electrons, basis = orb.shape
    depth = store.shape[1] // CHUNKS
    half = NY * CAP * electrons

    loads = [
        pltpu.make_async_copy(src, dst, load_sem.at[i])
        for i, (src, dst) in enumerate(((steps_hbm, stp), (cholesky_hbm, store.at[0]), (orbitals_hbm, orb)))
    ]
    for load in loads:
        load.start()

    up, down = {"x": lax.rem(x + 1, NX)}, {"x": lax.rem(x + NX - 1, NX)}
    peers = {
        "x+": up,
        "x-": down,
        "pair": {"l": 1 - l},
        "core": {"k": 1 - k},
        "y+": {"y": lax.rem(y + 1, NY)},
        "y-": {"y": lax.rem(y + NY - 1, NY)},
    }
    walk_ids = [(dh, dy) for dh in range(NH) for dy in (1, 3, 2, 0) if (dh, dy) != (0, 0)]
    walk_to = {(dh, dy): {"y": lax.rem(y + dy, NY), "h": lax.rem(h + dh, NH)} for dh, dy in walk_ids}
    walk_from = {(dh, dy): {"y": lax.rem(y + NY - dy, NY), "h": lax.rem(h + dh, NH)} for dh, dy in walk_ids}

    barrier = pltpu.get_barrier_semaphore()
    greeted = list(walk_to.values()) + [peers[p] for p in ("x+", "x-", "pair", "core")]
    for peer in greeted:
        pl.semaphore_signal(barrier, inc=1, device_id=peer, device_id_type=MESH)

    chol_walkers = 16 * per_device
    parent = [parents[0, j] for j in range(per_device)]
    owner = [p // chol_walkers for p in parent]
    keys = []
    for j in range(per_device):
        rank = sum([jnp.where(owner[i] == owner[j], 1, 0) for i in range(j)], jnp.int32(0))
        keys.append(owner[j] * CAP + rank)
    rows = lax.broadcasted_iota(jnp.int32, (per_device, 128), 0)
    loads[0].wait()
    walker_of, live_of = {}, {}
    for dh in range(NH):
        for dy in range(NY):
            device = lax.rem(y + dy, NY) * NH + lax.rem(h + dh, NH)
            for r in range(CAP):
                key = device * CAP + r
                index, mark, live = jnp.int32(0), jnp.int32(-1), jnp.int32(0)
                for j in range(per_device):
                    hit = keys[j] == key
                    alive = jnp.logical_and(hit, j < counts[0, 0])
                    index = jnp.where(hit, j, index)
                    mark = jnp.where(alive, parent[j] % per_device, mark)
                    live = jnp.where(alive, 1, live)
                walker_of[dh, dy, r], live_of[dh, dy, r] = index, live
                tag = jnp.where(rows == mark, 1.0, 0.0).astype(jnp.float32)
                if (dh, dy) == (0, 0):
                    slots[0, 0, r] = stp[index]
                    tags[0, 0, r] = tag
                else:
                    out[dh, dy, r] = stp[index]
                    tag_out[dh, dy, r] = tag
    loads[1].wait()
    pl.semaphore_wait(barrier, len(greeted))

    def remote(source, target, send, recv, peer):
        return pltpu.make_async_remote_copy(
            src_ref=source, dst_ref=target, send_sem=send, recv_sem=recv, device_id=peer, device_id_type=MESH
        )

    tag_copies, slot_copies = {}, {}
    for dh, dy in walk_ids:
        n, at = dh * NY + dy, (dh, dy)
        tag_copies[at] = remote(tag_out.at[at], tags.at[at], tag_send.at[n], tag_recv.at[n], walk_to[at])
        slot_copies[at] = remote(out.at[at], slots.at[at], slot_send.at[n], slot_recv.at[n], walk_to[at])
        tag_copies[at].start()
        slot_copies[at].start()

    links = Links(store, piece_send, piece_recv, peers, depth)

    def own(i):
        return store.at[0, pl.ds(lax.rem(y + i, CHUNKS) * depth, depth)]

    for i in range(CHUNKS):
        links.send(own(i), (BLOCK["H1"], i), "core")
        if i < 2:
            links.send(own(i), x_piece(0, 0, i, 0), "x+")
            links.send(own(i), x_piece(0, 1, i, 0), "x-")
    for i in range(2):
        links.send(own(i), pair_piece(i, 0), "pair")

    def x_arrived(dz, i):
        for side in range(2):
            piece = x_piece(dz, side, i, 0)
            links.wait(piece)
            links.forward(piece, x_piece(dz, side, i, 1), "core")

    def first_x():
        x_arrived(0, 0)

        @pl.when(k == 0)
        def _():
            links.forward(x_piece(0, 0, 0, 0), far_piece(0, 0, 0), "x+", "x")

        @pl.when(k == 1)
        def _():
            links.forward(x_piece(0, 1, 0, 0), far_piece(0, 0, 0), "x-", "x")

        for i in (2, 3):
            links.send(own(i), x_piece(0, 0, i, 0), "x+")
            links.send(own(i), x_piece(0, 1, i, 0), "x-")

    def pair_arrived(i):
        piece = pair_piece(i, 0)
        links.wait(piece)
        links.forward(piece, pair_piece(i, 1), "core")
        links.forward(piece, x_piece(1, 0, i, 0), "x+")
        links.forward(piece, x_piece(1, 1, i, 0), "x-")

    def far_arrived(dz):
        piece = far_piece(dz, 0, 0)
        links.wait(piece)
        links.forward(piece, far_piece(dz, 0, 1), "core")
        links.forward(piece, far_piece(dz, 3, 0), "y+")
        links.forward(piece, far_piece(dz, 1, 0), "y-")
        if dz == 0:
            links.forward(piece, far_piece(1, 0, 0), "pair")
            for i in (2, 3):
                links.send(own(i), pair_piece(i, 0), "pair")

    def far_turned(dz):
        for r, onward in ((3, "y+"), (1, "y-")):
            piece = far_piece(dz, r, 0)
            links.wait(piece)
            links.forward(piece, far_piece(dz, r, 1), "core")
            if (dz == 0) == (r == 3):
                links.forward(piece, far_piece(dz, 2, 0), onward)

    def far_last(dz):
        piece = far_piece(dz, 2, 0)
        links.wait(piece)
        links.forward(piece, far_piece(dz, 2, 1), "core")

    events = [
        (3, lambda: x_arrived(0, 1)),
        (6, lambda: far_arrived(0)),
        (7, lambda: pair_arrived(0)),
        (8, lambda: x_arrived(0, 2)),
        (9, lambda: pair_arrived(1)),
        (10, lambda: far_turned(0)),
        (12, lambda: x_arrived(0, 3)),
        (13, lambda: far_arrived(1)),
        (14, lambda: x_arrived(1, 0)),
        (15, lambda: pair_arrived(2)),
        (16, lambda: far_last(0)),
        (18, lambda: x_arrived(1, 1)),
        (19, lambda: pair_arrived(3)),
        (20, lambda: far_turned(1)),
        (22, lambda: far_last(1)),
        (26, lambda: x_arrived(1, 2)),
        (28, lambda: x_arrived(1, 3)),
    ]
    first_use = {}
    for place, name in enumerate(ORDER):
        first_use[name] = place if place < EARLY else 2 * place

    def clones(g):
        for dy in range(NY):
            if (g, dy) in slot_copies:
                tag_copies[g, dy].wait_recv()
                slot_copies[g, dy].wait_recv()

        def one_slot(s, carry):
            dy, r = s // CAP, s % CAP
            marks = [
                jnp.broadcast_to(tags[g, dy, r, i : i + 1, :], (16, 128)).astype(jnp.bfloat16) for i in range(per_device)
            ]
            for top in range(0, electrons, 16):
                for left in range(0, basis, 128):
                    found = jnp.zeros((16, 128), jnp.bfloat16)
                    for i in range(per_device):
                        found += orb[i, top : top + 16, left : left + 128] * marks[i]
                    step = slots[g, dy, r, top : top + 16, left : left + 128]
                    made = found.astype(jnp.float32) + step.astype(jnp.float32)
                    slots[g, dy, r, top : top + 16, left : left + 128] = made.astype(jnp.bfloat16)
            return carry

        lax.fori_loop(0, NY * CAP, one_slot, 0)
        turned[g] = slots[g].reshape(half, basis).T

    first_x()
    loads[2].wait()
    clones(0)
    total[...] = jnp.zeros_like(total)

    def with_events(t, carry):
        at = {}
        for when, event in events:
            at.setdefault(when, []).append(event)
        for name in ORDER[1:]:
            due = first_use[name]
            second = range(CHUNKS) if name == "H1" else (2, 3) if name[0] != "P" else (1, 3)
            pieces = [(BLOCK[name], m) for m in second]
            at.setdefault(due, []).append(lambda pieces=pieces: [links.wait(p) for p in pieces])
        for when in sorted(at):

            @pl.when(t == when)
            def _(when=when):
                for event in at[when]:
                    event()

        @pl.when(t == EARLY)
        def _():
            clones(1)

        half_step(store, turned, inter, total, t)
        return carry

    lax.fori_loop(0, 2 * len(ORDER), with_events, jnp.int32(0))

    def energy_of(s, carry):
        g, dy, r = s // (NY * CAP), s // CAP % NY, s % CAP
        base = pl.multiple_of((dy * CAP + r) * electrons, electrons)
        tile = jnp.zeros((8, 128), jnp.float32)
        for top in range(0, electrons, 16):
            for left in range(0, basis, 128):
                grad = total[g, pl.ds(base + top, 16), left : left + 128]
                made = slots[g, dy, r, top : top + 16, left : left + 128].astype(jnp.float32) * grad
                tile += made[:8] + made[8:]
        e_out[g, dy, r] = tile * -0.5
        return carry

    lax.fori_loop(0, NH * NY * CAP, energy_of, 0)
    e_copies = {}
    for dh, dy in walk_ids:
        n, at = dh * NY + dy, (dh, dy)
        e_copies[at] = remote(e_out.at[at], e_in.at[at], e_send.at[n], e_recv.at[n], walk_from[at])
        e_copies[at].start()

    for dh in range(NH):
        for dy in range(NY):
            for r in range(CAP):
                for i in range(per_device):
                    row = tags[dh, dy, r, i : i + 1, :]
                    weights[(dh * NY + dy) * CAP + r, i] = jnp.broadcast_to(-row, (8, 128))

    def gather(t, carry):
        top = pl.multiple_of(t // 8 * 8, 8)
        left = pl.multiple_of(t % 8 * 128, 128)
        sums = [jnp.zeros((8, 128), jnp.float32) for _ in range(per_device)]
        for s in range(NH * NY * CAP):
            g, at = s // (NY * CAP), s % (NY * CAP) * electrons
            grad = total[g, pl.ds(at + top, 8), pl.ds(left, 128)]
            for i in range(per_device):
                sums[i] += weights[s, i] * grad
        for i in range(per_device):
            grad_ref[i, pl.ds(top, 8), pl.ds(left, 128)] = sums[i]
        return carry

    lax.fori_loop(0, electrons * basis // 1024, gather, 0)

    for at in walk_ids:
        e_copies[at].wait()
    for j in range(per_device):
        tile = jnp.zeros((8, 128), jnp.float32)
        for dh in range(NH):
            for dy in range(NY):
                source = e_out if (dh, dy) == (0, 0) else e_in
                for r in range(CAP):
                    used = jnp.logical_and(walker_of[dh, dy, r] == j, live_of[dh, dy, r] == 1)
                    tile += jnp.where(used, 1.0, 0.0).astype(jnp.float32) * source[dh, dy, r]
        energy_ref[j] = tile

    for at in walk_ids:
        tag_copies[at].wait_send()
        slot_copies[at].wait_send()
    links.finish()


def body(orbitals, cholesky, parents, counts, steps):
    per_device, electrons, basis = orbitals.shape
    vectors = cholesky.shape[0]
    half = NY * CAP * electrons
    peers = (NH, NY)
    f32, bf16 = jnp.float32, jnp.bfloat16
    dma = pltpu.SemaphoreType.DMA
    energy, grad = pl.pallas_call(
        kernel,
        out_shape=(
            jax.ShapeDtypeStruct((per_device, 8, 128), f32),
            jax.ShapeDtypeStruct((per_device, electrons, basis), f32),
        ),
        in_specs=[pl.BlockSpec(memory_space=pltpu.SMEM)] * 2 + [pl.BlockSpec(memory_space=pl.ANY)] * 3,
        out_specs=(pl.BlockSpec(memory_space=pltpu.VMEM), pl.BlockSpec(memory_space=pltpu.VMEM)),
        scratch_shapes=[
            pltpu.VMEM((len(ORDER), vectors, electrons, basis), bf16),
            pltpu.VMEM((per_device, electrons, basis), bf16),
            pltpu.VMEM((per_device, electrons, basis), bf16),
            pltpu.VMEM((*peers, CAP, electrons, basis), bf16),
            pltpu.VMEM((*peers, CAP, electrons, basis), bf16),
            pltpu.VMEM((*peers, CAP, per_device, 128), f32),
            pltpu.VMEM((*peers, CAP, per_device, 128), f32),
            pltpu.VMEM((NH, basis, half), bf16),
            pltpu.VMEM((NH, half, basis), f32),
            pltpu.VMEM((half, vectors * electrons), bf16),
            pltpu.VMEM((NH * NY * CAP, per_device, 8, 128), f32),
            pltpu.VMEM((*peers, CAP, 8, 128), f32),
            pltpu.VMEM((*peers, CAP, 8, 128), f32),
            dma((3,)),
            *[dma((NH * NY,))] * 6,
            dma((64,)),
            dma((len(ORDER) * CHUNKS,)),
        ],
        compiler_params=pltpu.CompilerParams(
            collective_id=0, has_side_effects=True, vmem_limit_bytes=60 * 2**20
        ),
        name="exchange",
    )(parents.reshape(1, -1), counts, orbitals, cholesky, steps)
    return jnp.sum(energy, axis=(1, 2)), grad


def solution(mesh):
    torus = Mesh(mesh.devices.reshape(NY, NH, 2, NX, 2), NAMES)
    return jax.shard_map(
        body,
        mesh=torus,
        in_specs=(
            P(NAMES, None, None),
            P(("l", "x", "k"), None, None),
            P(NAMES),
            P(("y", "h"), ("l", "x", "k")),
            P(NAMES, None, None),
        ),
        out_specs=(P(NAMES), P(NAMES, None, None)),
        check_vma=False,
    )
```

time: 312 us -> 128 us (0.41)
  waiting for transfers between devices: 189 us -> 0 us
  Pallas kernels: 0 us -> 121 us
  matrix products: 56.6 us -> 0 us
  starting transfers between devices: 15 us -> 0 us
  between operations: 14.8 us -> 1.29 us
  local copies, waits for them, and re-layouts: 16.4 us -> 3.16 us
  blocking collectives: 8.93 us -> 0 us
  other arithmetic: 9.99 us -> 1.41 us
    pallas_call x0 -> x1, Pallas kernels: none -> 121 us  [body(): pl.pallas_call(kernel, out_shape=(jax.ShapeDtypeStruct((per_device, 8, 12...]
    all_gather x1 -> x0, waiting for transfers between devices: 98.2 us -> none  [body(): piece = lax.all_gather(cholesky, 'chol', axis=0, tiled=True)]
    all_to_all x3 -> x0, waiting for transfers between devices: 90.5 us -> none  [the longest x1 58.7 us: body(): lax.all_to_all(backward, WALK, split_axis=0, concat_axis=0, tiled=True)]
    dot_general x5 -> x0, matrix products: 56.6 us -> none  [the longest x1 47.7 us: body(): jnp.einsum('swgji,sgip->swjp', intersection, blocks, preferred_element_ty...]
    all_to_all x3 -> x0, starting transfers between devices: 15 us -> none  [the longest x1 6.27 us: body(): lax.all_to_all(backward, WALK, split_axis=0, concat_axis=0, tiled=True)]
    all_to_all x1 -> x0, blocking collectives: 8.93 us -> none  [turned_blocks(): lax.all_to_all(parts, axes[k], split_axis=k, concat_axis=k, tiled=True)]
    unnamed x12 -> x1, local copies, waits for them, and re-layouts: 11 us -> 3.16 us
    reduce_sum x4 -> x1, other arithmetic: 8.54 us -> 1.41 us  [body(): return (jnp.sum(energy, axis=(1, 2)), grad)]
  transfers between devices with their start and end apart: 4 -> 0, of which waited for: 4 -> 0; matrix products, arithmetic and copies ran while one was open for 3% -> 0% of each run, Pallas kernels for 0% -> 0%
where the time goes in v1:
time: 128 us; the launch traced here: 126 us
  Pallas kernels  121 us (95%)
  local copies, waits for them, and re-layouts  3.16 us (2%)
  other arithmetic  1.41 us (1%)
  between operations  1.29 us (1%)
    pallas_call x1, Pallas kernels, body(): pl.pallas_call(kernel, out_shape=(jax.ShapeDtypeStruct((per_device, 8, 12...  121 us
    unnamed x1, local copies, waits for them, and re-layouts  3.16 us

profile of v1, /device:TPU:1, one launch (start us, length us, event | category | flops | bytes accessed | tf_op | source)
XLA Modules:
  0.0 126.5 jit_solution(9856152739301772614)
XLA Ops:
  1.3 120.6 %exchange.1 = (f32[8,8,128]{2,1,0:T(8,128)}, f32[8,64,1024]{2,1,0:T(8,128)}) custom-call(s32[1,8]{1,0:T(1,128)} %bitcast.1, s32[1,1]{1,0:T(1,128)S(6)} %copy.8.counts, bf16[8,64,1024]{2,1,0:T(8,128)(2,1)} %orbitals_hbm.1, bf16[12,64,1024]{2,1,0:T(8,128)(2,1)} %cholesky_hbm.1, bf16[8,64,1024]{2,1,0:T(8,128)(2,1)} %steps_hbm.1), custom_call_target="tpu_custom_call" | custom-call | tf_op jit(solution)/shard_map/exchange/pallas_call | solution.py:392
  121.9 1.4 %reduce_sum.9 = f32[8]{0:T(128)} reduce(f32[8,8,128]{2,1,0:T(8,128)} %get-tuple-element.4, f32[]{:T(128)} %constant.0.clone.1), dimensions={1,2}, to_apply=%region_0.0 | reduce | flops 8184 | bytes 32804 | tf_op jit(solution)/shard_map/reduce_sum | solution.py:424
  123.3 3.2 %copy.9 = f32[8,64,1024]{2,1,0:T(8,128)} copy(f32[8,64,1024]{2,1,0:T(8,128)} %get-tuple-element.9) | data formatting | bytes 4194304

commit v2 on v1

v2 whole, which is shorter than its diff:
```python
import functools

import jax
import jax.numpy as jnp
from jax import lax
from jax.experimental import pallas as pl
from jax.experimental.pallas import tpu as pltpu
from jax.sharding import Mesh
from jax.sharding import PartitionSpec as P

NAMES = ("y", "h", "l", "x", "k")
MESH = pl.DeviceIdType.MESH
CAP = 2
NY, NH, NX = 4, 2, 4
CHUNKS = 4
EARLY = 5

REACH = ((0, 0), (0, 1), (0, 3), (1, 0), (0, 2), (1, 1), (1, 3), (1, 2))

ORDER = ("H0", "H1", "X00", "X01", "X02", "X03", "P1", "P0", "X11", "O0", "X10", "X12", "O1", "X13", "O3", "O2")
BLOCK = {name: i for i, name in enumerate(ORDER)}


def pair_piece(i, dk):
    return (BLOCK[f"P{i // 2}"], (i % 2) * 2 + dk)


def x_piece(dz, side, i, dk):
    return (BLOCK[f"X{dz}{i}"], side + 2 * dk)


def far_piece(dz, r, dk):
    return (BLOCK[f"O{r}"], dz + 2 * dk)


def piece_id(piece):
    return piece[0] * CHUNKS + piece[1]


class Links:
    def __init__(self, store, send_sem, recv_sem, peers, depth):
        self.store, self.send_sem, self.recv_sem = store, send_sem, recv_sem
        self.peers, self.depth = peers, depth
        self.sends = {}

    def view(self, piece):
        return self.store.at[piece[0], pl.ds(piece[1] * self.depth, self.depth)]

    def send(self, source, piece, peer, key=None):
        copy = pltpu.make_async_remote_copy(
            src_ref=source,
            dst_ref=self.view(piece),
            send_sem=self.send_sem.at[self.sends.setdefault((piece, key or peer), len(self.sends))],
            recv_sem=self.recv_sem.at[piece_id(piece)],
            device_id=self.peers[peer],
            device_id_type=MESH,
        )
        copy.start()

    def forward(self, piece, target, peer, key=None):
        self.send(self.view(piece), target, peer, key)

    def any_copy(self, piece, send_sem, recv_sem):
        here = self.view(piece)
        return pltpu.make_async_remote_copy(
            src_ref=here,
            dst_ref=here,
            send_sem=send_sem,
            recv_sem=recv_sem,
            device_id=self.peers["core"],
            device_id_type=MESH,
        )

    def wait(self, piece):
        self.any_copy(piece, self.send_sem.at[0], self.recv_sem.at[piece_id(piece)]).wait_recv()

    def finish(self):
        for n in range(len(self.sends)):
            self.any_copy((0, 0), self.send_sem.at[n], self.recv_sem.at[0]).wait_send()


def half_step(store, turned, inter, total, t):
    electrons, basis = store.shape[2:]
    early, late = t < EARLY, t < 2 * EARLY
    g = jnp.where(late, jnp.where(early, 0, 1), lax.rem(t, 2))
    b = jnp.where(late, jnp.where(early, t, t - EARLY), t // 2)
    block = store.at[b]
    for n in range(turned.shape[2] // 256):
        for m in range(store.shape[1] // 4):
            vectors = block[4 * m : 4 * m + 4].reshape(4 * electrons, basis)
            made = jnp.dot(vectors, turned[g, :, n * 256 : (n + 1) * 256], preferred_element_type=jnp.float32)
            made = made.astype(jnp.bfloat16)
            for v in range(0, 4, 2):
                for s in range(0, 4, 2):
                    a = made[v * 64 : v * 64 + 64, s * 64 : s * 64 + 128]
                    c = made[v * 64 + 64 : v * 64 + 128, s * 64 : s * 64 + 128]
                    row, col = (4 * n + s) * 64, (4 * m + v) * 64
                    inter[row : row + 64, col : col + 128] = jnp.concatenate([a[:, :64], c[:, :64]], axis=1)
                    inter[row + 64 : row + 128, col : col + 128] = jnp.concatenate([a[:, 64:], c[:, 64:]], axis=1)
    for n in range(basis // 256):
        part = block[:, :, n * 256 : (n + 1) * 256].reshape(-1, 256)
        total[g, :, n * 256 : (n + 1) * 256] += jnp.dot(inter[...], part, preferred_element_type=jnp.float32)


def kernel(
    parents, counts, orbitals_hbm, cholesky_hbm, steps_hbm, energy_ref, grad_ref,
    store, orb, stp, out, slots, tag_out, tags, turned, total, inter, weights, e_out, e_in,
    load_sem, slot_send, slot_recv, tag_send, tag_recv, e_send, e_recv, piece_send, piece_recv,
):
    y, h, l, x, k = (lax.axis_index(name) for name in NAMES)
    per_device, electrons, basis = orb.shape
    depth = store.shape[1] // CHUNKS
    half = NY * CAP * electrons

    loads = [
        pltpu.make_async_copy(src, dst, load_sem.at[i])
        for i, (src, dst) in enumerate(((steps_hbm, stp), (cholesky_hbm, store.at[0]), (orbitals_hbm, orb)))
    ]
    for load in loads:
        load.start()

    up, down = {"x": lax.rem(x + 1, NX)}, {"x": lax.rem(x + NX - 1, NX)}
    peers = {
        "x+": up,
        "x-": down,
        "pair": {"l": 1 - l},
        "cross": {"h": 1 - h, "l": 1 - l},
        "core": {"k": 1 - k},
        "y+": {"y": lax.rem(y + 1, NY)},
        "y-": {"y": lax.rem(y + NY - 1, NY)},
    }
    walk_ids = range(1, len(REACH))
    walk_to = {n: {"y": lax.rem(y + REACH[n][1], NY), "h": lax.rem(h + REACH[n][0], NH)} for n in walk_ids}
    walk_from = {n: {"y": lax.rem(y + NY - REACH[n][1], NY), "h": lax.rem(h + REACH[n][0], NH)} for n in walk_ids}

    barrier = pltpu.get_barrier_semaphore()
    greeted = list(walk_to.values()) + [peers[p] for p in ("x+", "x-", "pair", "cross", "core")]
    for peer in greeted:
        pl.semaphore_signal(barrier, inc=1, device_id=peer, device_id_type=MESH)

    chol_walkers = 16 * per_device
    parent = [parents[0, j] for j in range(per_device)]
    owner = [p // chol_walkers for p in parent]
    keys = []
    for j in range(per_device):
        rank = sum([jnp.where(owner[i] == owner[j], 1, 0) for i in range(j)], jnp.int32(0))
        keys.append(owner[j] * CAP + rank)
    rows = lax.broadcasted_iota(jnp.int32, (per_device, 128), 0)
    loads[0].wait()
    walker_of, live_of = {}, {}
    for n, (dh, dy) in enumerate(REACH):
        device = lax.rem(y + dy, NY) * NH + lax.rem(h + dh, NH)
        for r in range(CAP):
            key = device * CAP + r
            index, mark, live = jnp.int32(0), jnp.int32(-1), jnp.int32(0)
            for j in range(per_device):
                hit = keys[j] == key
                alive = jnp.logical_and(hit, j < counts[0, 0])
                index = jnp.where(hit, j, index)
                mark = jnp.where(alive, parent[j] % per_device, mark)
                live = jnp.where(alive, 1, live)
            walker_of[n, r], live_of[n, r] = index, live
            tag = jnp.where(rows == mark, 1.0, 0.0).astype(jnp.float32)
            (out if n else slots)[n, r] = stp[index]
            (tag_out if n else tags)[n, r] = tag
    loads[1].wait()
    pl.semaphore_wait(barrier, len(greeted))

    def remote(source, target, send, recv, peer):
        return pltpu.make_async_remote_copy(
            src_ref=source, dst_ref=target, send_sem=send, recv_sem=recv, device_id=peer, device_id_type=MESH
        )

    tag_copies, slot_copies = {}, {}
    for n in walk_ids:
        tag_copies[n] = remote(tag_out.at[n], tags.at[n], tag_send.at[n], tag_recv.at[n], walk_to[n])
        slot_copies[n] = remote(out.at[n], slots.at[n], slot_send.at[n], slot_recv.at[n], walk_to[n])
        tag_copies[n].start()
        slot_copies[n].start()

    links = Links(store, piece_send, piece_recv, peers, depth)

    def own(i):
        return store.at[0, pl.ds(lax.rem(y + i, CHUNKS) * depth, depth)]

    for i in range(CHUNKS):
        links.send(own(i), (BLOCK["H1"], i), "core")
        links.send(own(i), x_piece(0, 0, i, 0), "x+")
        links.send(own(i), x_piece(0, 1, i, 0), "x-")
    links.send(own(1), pair_piece(1, 0), "pair")
    links.send(own(0), pair_piece(0, 0), "pair")
    links.send(own(2), pair_piece(2, 0), "cross")
    links.send(own(3), pair_piece(3, 0), "cross")

    def x_arrived(dz, i):
        for side in range(2):
            piece = x_piece(dz, side, i, 0)
            links.wait(piece)
            links.forward(piece, x_piece(dz, side, i, 1), "core")

    def first_x():
        x_arrived(0, 0)

        @pl.when(k == 0)
        def _():
            links.forward(x_piece(0, 0, 0, 0), far_piece(0, 0, 0), "x+", "x")

        @pl.when(k == 1)
        def _():
            links.forward(x_piece(0, 1, 0, 0), far_piece(0, 0, 0), "x-", "x")

        for side in range(2):
            links.forward(x_piece(0, side, 0, 0), x_piece(1, side, 0, 0), "cross")

    def pair_arrived(i):
        piece = pair_piece(i, 0)
        links.wait(piece)
        links.forward(piece, pair_piece(i, 1), "core")
        if i:
            links.forward(piece, x_piece(1, 0, i, 0), "x+")
            links.forward(piece, x_piece(1, 1, i, 0), "x-")

    def far_arrived(dz):
        piece = far_piece(dz, 0, 0)
        links.wait(piece)
        links.forward(piece, far_piece(dz, 0, 1), "core")
        links.forward(piece, far_piece(dz, 3, 0), "y+")
        links.forward(piece, far_piece(dz, 1, 0), "y-")
        if dz == 0:
            links.forward(piece, far_piece(1, 0, 0), "pair")

    def far_turned(dz):
        for r, onward in ((3, "y+"), (1, "y-")):
            piece = far_piece(dz, r, 0)
            links.wait(piece)
            links.forward(piece, far_piece(dz, r, 1), "core")
            if (dz == 0) == (r == 3):
                links.forward(piece, far_piece(dz, 2, 0), onward)

    def far_last(dz):
        piece = far_piece(dz, 2, 0)
        links.wait(piece)
        links.forward(piece, far_piece(dz, 2, 1), "core")

    events = [
        (1, first_x, ()),
        (3, x_arrived, (0, 1)),
        (4, x_arrived, (0, 2)),
        (6, pair_arrived, (1,)),
        (6, pair_arrived, (2,)),
        (7, x_arrived, (0, 3)),
        (10, pair_arrived, (0,)),
        (10, pair_arrived, (3,)),
        (11, far_arrived, (0,)),
        (14, x_arrived, (1, 1)),
        (16, far_arrived, (1,)),
        (17, far_turned, (0,)),
        (18, x_arrived, (1, 0)),
        (20, x_arrived, (1, 2)),
        (22, far_turned, (1,)),
        (24, x_arrived, (1, 3)),
        (25, far_last, (0,)),
        (28, far_last, (1,)),
    ]
    first_use = {}
    for place, name in enumerate(ORDER):
        first_use[name] = place if place < EARLY else 2 * place

    per_half = len(REACH) // 2

    def clones(g):
        for n in range(g * per_half, (g + 1) * per_half):
            if n:
                tag_copies[n].wait_recv()
                slot_copies[n].wait_recv()

        def one_slot(s, carry):
            n, r = g * per_half + s // CAP, s % CAP
            marks = [
                jnp.broadcast_to(tags[n, r, i : i + 1, :], (16, 128)).astype(jnp.bfloat16) for i in range(per_device)
            ]
            for top in range(0, electrons, 16):
                for left in range(0, basis, 128):
                    found = jnp.zeros((16, 128), jnp.bfloat16)
                    for i in range(per_device):
                        found += orb[i, top : top + 16, left : left + 128] * marks[i]
                    step = slots[n, r, top : top + 16, left : left + 128]
                    made = found.astype(jnp.float32) + step.astype(jnp.float32)
                    slots[n, r, top : top + 16, left : left + 128] = made.astype(jnp.bfloat16)
            return carry

        lax.fori_loop(0, per_half * CAP, one_slot, 0)
        turned[g] = slots[g * per_half : (g + 1) * per_half].reshape(half, basis).T

    loads[2].wait()
    clones(0)
    total[...] = jnp.zeros_like(total)

    at = {}
    for when, event, of in events:
        at.setdefault(when, []).append(functools.partial(event, *of))
    for name in ORDER[1:]:
        second = range(CHUNKS) if name == "H1" else (1, 3) if name[0] == "P" else (2, 3)
        for m in second:
            at.setdefault(first_use[name], []).append(functools.partial(links.wait, (BLOCK[name], m)))
    at.setdefault(EARLY, []).append(functools.partial(clones, 1))

    def dispatch(t, first, last):
        due = [when for when in at if first <= when < last]
        if not due:
            return
        if last - first == 1:
            for event in at[first]:
                event()
            return
        middle = (first + last) // 2
        if min(due) < middle:
            pl.when(t < middle)(lambda: dispatch(t, first, middle))
        if max(due) >= middle:
            pl.when(t >= middle)(lambda: dispatch(t, middle, last))

    def with_events(t, carry):
        dispatch(t, 0, 2 * len(ORDER))
        half_step(store, turned, inter, total, t)
        return carry

    lax.fori_loop(0, 2 * len(ORDER), with_events, jnp.int32(0))

    def energy_of(s, carry):
        n, r = s // CAP, s % CAP
        g = n // per_half
        base = pl.multiple_of(s % (per_half * CAP) * electrons, electrons)
        tile = jnp.zeros((8, 128), jnp.float32)
        for top in range(0, electrons, 16):
            for left in range(0, basis, 128):
                grad = total[g, pl.ds(base + top, 16), left : left + 128]
                made = slots[n, r, top : top + 16, left : left + 128].astype(jnp.float32) * grad
                tile += made[:8] + made[8:]
        e_out[n, r] = tile * -0.5
        return carry

    lax.fori_loop(0, len(REACH) * CAP, energy_of, 0)
    e_copies = {}
    for n in walk_ids:
        e_copies[n] = remote(e_out.at[n], e_in.at[n], e_send.at[n], e_recv.at[n], walk_from[n])
        e_copies[n].start()

    for n in range(len(REACH)):
        for r in range(CAP):
            for i in range(per_device):
                weights[n * CAP + r, i] = jnp.broadcast_to(-tags[n, r, i : i + 1, :], (8, 128))

    def gather(t, carry):
        top = pl.multiple_of(t // 8 * 8, 8)
        left = pl.multiple_of(t % 8 * 128, 128)
        sums = [jnp.zeros((8, 128), jnp.float32) for _ in range(per_device)]
        for s in range(len(REACH) * CAP):
            g, first = s // (per_half * CAP), s % (per_half * CAP) * electrons
            grad = total[g, pl.ds(first + top, 8), pl.ds(left, 128)]
            for i in range(per_device):
                sums[i] += weights[s, i] * grad
        for i in range(per_device):
            grad_ref[i, pl.ds(top, 8), pl.ds(left, 128)] = sums[i]
        return carry

    lax.fori_loop(0, electrons * basis // 1024, gather, 0)

    for n in walk_ids:
        e_copies[n].wait()
    for j in range(per_device):
        tile = jnp.zeros((8, 128), jnp.float32)
        for n in range(len(REACH)):
            for r in range(CAP):
                used = jnp.logical_and(walker_of[n, r] == j, live_of[n, r] == 1)
                tile += jnp.where(used, 1.0, 0.0).astype(jnp.float32) * (e_in if n else e_out)[n, r]
        energy_ref[j] = tile

    for n in walk_ids:
        tag_copies[n].wait_send()
        slot_copies[n].wait_send()
    links.finish()


def body(orbitals, cholesky, parents, counts, steps):
    per_device, electrons, basis = orbitals.shape
    vectors = cholesky.shape[0]
    half = NY * CAP * electrons
    reach = len(REACH)
    f32, bf16 = jnp.float32, jnp.bfloat16
    dma = pltpu.SemaphoreType.DMA
    energy, grad = pl.pallas_call(
        kernel,
        out_shape=(
            jax.ShapeDtypeStruct((per_device, 8, 128), f32),
            jax.ShapeDtypeStruct((per_device, electrons, basis), f32),
        ),
        in_specs=[pl.BlockSpec(memory_space=pltpu.SMEM)] * 2 + [pl.BlockSpec(memory_space=pl.ANY)] * 3,
        out_specs=(pl.BlockSpec(memory_space=pltpu.VMEM), pl.BlockSpec(memory_space=pltpu.VMEM)),
        scratch_shapes=[
            pltpu.VMEM((len(ORDER), vectors, electrons, basis), bf16),
            pltpu.VMEM((per_device, electrons, basis), bf16),
            pltpu.VMEM((per_device, electrons, basis), bf16),
            pltpu.VMEM((reach, CAP, electrons, basis), bf16),
            pltpu.VMEM((reach, CAP, electrons, basis), bf16),
            pltpu.VMEM((reach, CAP, per_device, 128), f32),
            pltpu.VMEM((reach, CAP, per_device, 128), f32),
            pltpu.VMEM((2, basis, half), bf16),
            pltpu.VMEM((2, half, basis), f32),
            pltpu.VMEM((half, vectors * electrons), bf16),
            pltpu.VMEM((reach * CAP, per_device, 8, 128), f32),
            pltpu.VMEM((reach, CAP, 8, 128), f32),
            pltpu.VMEM((reach, CAP, 8, 128), f32),
            dma((3,)),
            *[dma((reach,))] * 6,
            dma((64,)),
            dma((len(ORDER) * CHUNKS,)),
        ],
        compiler_params=pltpu.CompilerParams(
            collective_id=0, has_side_effects=True, vmem_limit_bytes=60 * 2**20
        ),
        name="exchange",
    )(parents.reshape(1, -1), counts, orbitals, cholesky, steps)
    return jnp.sum(energy, axis=(1, 2)), grad


def solution(mesh):
    torus = Mesh(mesh.devices.reshape(NY, NH, 2, NX, 2), NAMES)
    return jax.shard_map(
        body,
        mesh=torus,
        in_specs=(
            P(NAMES, None, None),
            P(("l", "x", "k"), None, None),
            P(NAMES),
            P(("y", "h"), ("l", "x", "k")),
            P(NAMES, None, None),
        ),
        out_specs=(P(NAMES), P(NAMES, None, None)),
        check_vma=False,
    )
```

time: 128 us -> 110 us (0.86)
  Pallas kernels: 121 us -> 104 us
    pallas_call x1, Pallas kernels: 121 us -> 104 us  [body(): pl.pallas_call(kernel, out_shape=(jax.ShapeDtypeStruct((per_device, 8, 12...]
where the time goes in v2:
time: 110 us
  Pallas kernels  104 us (95%)
  local copies, waits for them, and re-layouts  3.16 us (3%)
  other arithmetic  1.41 us (1%)
  between operations  1.29 us (1%)
    pallas_call x1, Pallas kernels, body(): pl.pallas_call(kernel, out_shape=(jax.ShapeDtypeStruct((per_device, 8, 12...  104 us
    unnamed x1, local copies, waits for them, and re-layouts  3.16 us

profile of v2, /device:TPU:1, one launch (start us, length us, event | category | flops | bytes accessed | tf_op | source)
XLA Modules:
  0.0 109.7 jit_solution(7679355281056795439)
XLA Ops:
  1.3 103.9 %exchange.1 = (f32[8,8,128]{2,1,0:T(8,128)}, f32[8,64,1024]{2,1,0:T(8,128)}) custom-call(s32[1,8]{1,0:T(1,128)} %bitcast.1, s32[1,1]{1,0:T(1,128)S(6)} %copy.8.counts, bf16[8,64,1024]{2,1,0:T(8,128)(2,1)} %orbitals_hbm.1, bf16[12,64,1024]{2,1,0:T(8,128)(2,1)} %cholesky_hbm.1, bf16[8,64,1024]{2,1,0:T(8,128)(2,1)} %steps_hbm.1), custom_call_target="tpu_custom_call" | custom-call | tf_op jit(solution)/shard_map/exchange/pallas_call | solution.py:391
  105.1 1.4 %reduce_sum.9 = f32[8]{0:T(128)} reduce(f32[8,8,128]{2,1,0:T(8,128)} %get-tuple-element.4, f32[]{:T(128)} %constant.0.clone.1), dimensions={1,2}, to_apply=%region_0.0 | reduce | flops 8184 | bytes 32804 | tf_op jit(solution)/shard_map/reduce_sum | solution.py:423
  106.6 3.2 %copy.9 = f32[8,64,1024]{2,1,0:T(8,128)} copy(f32[8,64,1024]{2,1,0:T(8,128)} %get-tuple-element.9) | data formatting | bytes 4194304

commit v3 on v2

--- a/solution.py
+++ b/solution.py
@@ -13,7 +13,7 @@
 CAP = 2
 NY, NH, NX = 4, 2, 4
 CHUNKS = 4
-EARLY = 5
+EARLY = 4
 
 REACH = ((0, 0), (0, 1), (0, 3), (1, 0), (0, 2), (1, 1), (1, 3), (1, 2))
 
@@ -79,15 +79,11 @@
             self.any_copy((0, 0), self.send_sem.at[n], self.recv_sem.at[0]).wait_send()
 
 
-def half_step(store, turned, inter, total, t):
-    electrons, basis = store.shape[2:]
-    early, late = t < EARLY, t < 2 * EARLY
-    g = jnp.where(late, jnp.where(early, 0, 1), lax.rem(t, 2))
-    b = jnp.where(late, jnp.where(early, t, t - EARLY), t // 2)
-    block = store.at[b]
+def meet(block, turned, inter, g):
+    electrons = block.shape[1]
     for n in range(turned.shape[2] // 256):
-        for m in range(store.shape[1] // 4):
-            vectors = block[4 * m : 4 * m + 4].reshape(4 * electrons, basis)
+        for m in range(block.shape[0] // 4):
+            vectors = block[4 * m : 4 * m + 4].reshape(4 * electrons, -1)
             made = jnp.dot(vectors, turned[g, :, n * 256 : (n + 1) * 256], preferred_element_type=jnp.float32)
             made = made.astype(jnp.bfloat16)
             for v in range(0, 4, 2):
@@ -95,16 +91,19 @@
                     a = made[v * 64 : v * 64 + 64, s * 64 : s * 64 + 128]
                     c = made[v * 64 + 64 : v * 64 + 128, s * 64 : s * 64 + 128]
                     row, col = (4 * n + s) * 64, (4 * m + v) * 64
-                    inter[row : row + 64, col : col + 128] = jnp.concatenate([a[:, :64], c[:, :64]], axis=1)
-                    inter[row + 64 : row + 128, col : col + 128] = jnp.concatenate([a[:, 64:], c[:, 64:]], axis=1)
-    for n in range(basis // 256):
+                    inter[g, row : row + 64, col : col + 128] = jnp.concatenate([a[:, :64], c[:, :64]], axis=1)
+                    inter[g, row + 64 : row + 128, col : col + 128] = jnp.concatenate([a[:, 64:], c[:, 64:]], axis=1)
+
+
+def spread(block, inter, total, g):
+    for n in range(block.shape[2] // 256):
         part = block[:, :, n * 256 : (n + 1) * 256].reshape(-1, 256)
-        total[g, :, n * 256 : (n + 1) * 256] += jnp.dot(inter[...], part, preferred_element_type=jnp.float32)
+        total[g, :, n * 256 : (n + 1) * 256] += jnp.dot(inter[g], part, preferred_element_type=jnp.float32)
 
 
 def kernel(
     parents, counts, orbitals_hbm, cholesky_hbm, steps_hbm, energy_ref, grad_ref,
-    store, orb, stp, out, slots, tag_out, tags, turned, total, inter, weights, e_out, e_in,
+    store, orb, stp, out, slots, tag_out, tags, turned, total, inter, weights, made_grad, e_out, e_in,
     load_sem, slot_send, slot_recv, tag_send, tag_recv, e_send, e_recv, piece_send, piece_recv,
 ):
     y, h, l, x, k = (lax.axis_index(name) for name in NAMES)
@@ -248,18 +247,18 @@
         (4, x_arrived, (0, 2)),
         (6, pair_arrived, (1,)),
         (6, pair_arrived, (2,)),
-        (7, x_arrived, (0, 3)),
-        (10, pair_arrived, (0,)),
-        (10, pair_arrived, (3,)),
-        (11, far_arrived, (0,)),
-        (14, x_arrived, (1, 1)),
+        (8, x_arrived, (0, 3)),
+        (11, pair_arrived, (0,)),
+        (11, pair_arrived, (3,)),
+        (12, far_arrived, (0,)),
+        (15, x_arrived, (1, 1)),
         (16, far_arrived, (1,)),
         (17, far_turned, (0,)),
-        (18, x_arrived, (1, 0)),
+        (19, x_arrived, (1, 0)),
         (20, x_arrived, (1, 2)),
         (22, far_turned, (1,)),
-        (24, x_arrived, (1, 3)),
-        (25, far_last, (0,)),
+        (23, x_arrived, (1, 3)),
+        (26, far_last, (0,)),
         (28, far_last, (1,)),
     ]
     first_use = {}
@@ -269,28 +268,30 @@
     per_half = len(REACH) // 2
 
     def clones(g):
-        for n in range(g * per_half, (g + 1) * per_half):
+        for place in range(per_half):
+            n = g * per_half + place
             if n:
                 tag_copies[n].wait_recv()
                 slot_copies[n].wait_recv()
 
-        def one_slot(s, carry):
-            n, r = g * per_half + s // CAP, s % CAP
-            marks = [
-                jnp.broadcast_to(tags[n, r, i : i + 1, :], (16, 128)).astype(jnp.bfloat16) for i in range(per_device)
-            ]
-            for top in range(0, electrons, 16):
-                for left in range(0, basis, 128):
-                    found = jnp.zeros((16, 128), jnp.bfloat16)
-                    for i in range(per_device):
-                        found += orb[i, top : top + 16, left : left + 128] * marks[i]
-                    step = slots[n, r, top : top + 16, left : left + 128]
-                    made = found.astype(jnp.float32) + step.astype(jnp.float32)
-                    slots[n, r, top : top + 16, left : left + 128] = made.astype(jnp.bfloat16)
-            return carry
-
-        lax.fori_loop(0, per_half * CAP, one_slot, 0)
-        turned[g] = slots[g * per_half : (g + 1) * per_half].reshape(half, basis).T
+            def one_slot(r, carry, n=n):
+                marks = [
+                    jnp.broadcast_to(tags[n, r, i : i + 1, :], (16, 128)).astype(jnp.bfloat16)
+                    for i in range(per_device)
+                ]
+                for top in range(0, electrons, 16):
+                    for left in range(0, basis, 128):
+                        found = jnp.zeros((16, 128), jnp.bfloat16)
+                        for i in range(per_device):
+                            found += orb[i, top : top + 16, left : left + 128] * marks[i]
+                        step = slots[n, r, top : top + 16, left : left + 128]
+                        made = found.astype(jnp.float32) + step.astype(jnp.float32)
+                        slots[n, r, top : top + 16, left : left + 128] = made.astype(jnp.bfloat16)
+                return carry
+
+            lax.fori_loop(0, CAP, one_slot, 0)
+            wide = CAP * electrons
+            turned[g, :, place * wide : (place + 1) * wide] = slots[n].reshape(wide, basis).T
 
     loads[2].wait()
     clones(0)
@@ -305,7 +306,31 @@
             at.setdefault(first_use[name], []).append(functools.partial(links.wait, (BLOCK[name], m)))
     at.setdefault(EARLY, []).append(functools.partial(clones, 1))
 
-    def dispatch(t, first, last):
+    e_copies = {
+        n: remote(e_out.at[n], e_in.at[n], e_send.at[n], e_recv.at[n], walk_from[n]) for n in walk_ids
+    }
+
+    def energies(g):
+        def energy_of(s, carry):
+            n, r = s // CAP, s % CAP
+            base = pl.multiple_of(s % (per_half * CAP) * electrons, electrons)
+            tile = jnp.zeros((8, 128), jnp.float32)
+            for top in range(0, electrons, 16):
+                for left in range(0, basis, 128):
+                    grad = total[g, pl.ds(base + top, 16), left : left + 128]
+                    made = slots[n, r, top : top + 16, left : left + 128].astype(jnp.float32) * grad
+                    tile += made[:8] + made[8:]
+            e_out[n, r] = tile * -0.5
+            return carry
+
+        lax.fori_loop(g * per_half * CAP, (g + 1) * per_half * CAP, energy_of, 0)
+        for n in range(g * per_half, (g + 1) * per_half):
+            if n:
+                e_copies[n].start()
+
+    at.setdefault(2 * len(ORDER) - 1, []).append(functools.partial(energies, 1))
+
+    def dispatch(t, at, first, last):
         due = [when for when in at if first <= when < last]
         if not due:
             return
@@ -315,36 +340,35 @@
             return
         middle = (first + last) // 2
         if min(due) < middle:
-            pl.when(t < middle)(lambda: dispatch(t, first, middle))
+            pl.when(t < middle)(lambda: dispatch(t, at, first, middle))
         if max(due) >= middle:
-            pl.when(t >= middle)(lambda: dispatch(t, middle, last))
-
-    def with_events(t, carry):
-        dispatch(t, 0, 2 * len(ORDER))
-        half_step(store, turned, inter, total, t)
+            pl.when(t >= middle)(lambda: dispatch(t, at, middle, last))
+
+    def half_step(t, carry):
+        dispatch(t, at, 0, 2 * EARLY)
+        g = jnp.where(t < EARLY, 0, 1)
+        block = store.at[jnp.where(t < EARLY, t, t - EARLY)]
+        meet(block, turned, inter, g)
+        spread(block, inter, total, g)
         return carry
 
-    lax.fori_loop(0, 2 * len(ORDER), with_events, jnp.int32(0))
-
-    def energy_of(s, carry):
-        n, r = s // CAP, s % CAP
-        g = n // per_half
-        base = pl.multiple_of(s % (per_half * CAP) * electrons, electrons)
-        tile = jnp.zeros((8, 128), jnp.float32)
-        for top in range(0, electrons, 16):
-            for left in range(0, basis, 128):
-                grad = total[g, pl.ds(base + top, 16), left : left + 128]
-                made = slots[n, r, top : top + 16, left : left + 128].astype(jnp.float32) * grad
-                tile += made[:8] + made[8:]
-        e_out[n, r] = tile * -0.5
+    opening = {when // 2: at[when] for when in at if when >= 2 * EARLY and when % 2 == 0}
+    middle = {when // 2: at[when] for when in at if when >= 2 * EARLY and when % 2 == 1}
+
+    def full_step(b, carry):
+        dispatch(b, opening, EARLY, len(ORDER))
+        block = store.at[b]
+        meet(block, turned, inter, 1)
+        meet(block, turned, inter, 0)
+        spread(block, inter, total, 1)
+        dispatch(b, middle, EARLY, len(ORDER))
+        spread(block, inter, total, 0)
         return carry
 
-    lax.fori_loop(0, len(REACH) * CAP, energy_of, 0)
-    e_copies = {}
-    for n in walk_ids:
-        e_copies[n] = remote(e_out.at[n], e_in.at[n], e_send.at[n], e_recv.at[n], walk_from[n])
-        e_copies[n].start()
-
+    lax.fori_loop(0, 2 * EARLY, half_step, jnp.int32(0))
+    lax.fori_loop(EARLY, len(ORDER), full_step, jnp.int32(0))
+
+    energies(0)
     for n in range(len(REACH)):
         for r in range(CAP):
             for i in range(per_device):
@@ -360,11 +384,17 @@
             for i in range(per_device):
                 sums[i] += weights[s, i] * grad
         for i in range(per_device):
-            grad_ref[i, pl.ds(top, 8), pl.ds(left, 128)] = sums[i]
+            made_grad[i, pl.ds(top, 8), pl.ds(left, 128)] = sums[i]
         return carry
 
     lax.fori_loop(0, electrons * basis // 1024, gather, 0)
 
+    store_grad = pltpu.make_async_copy(made_grad, grad_ref, load_sem.at[0])
+    store_grad.start()
+    for n in walk_ids:
+        tag_copies[n].wait_send()
+        slot_copies[n].wait_send()
+    links.finish()
     for n in walk_ids:
         e_copies[n].wait()
     for j in range(per_device):
@@ -375,10 +405,19 @@
                 tile += jnp.where(used, 1.0, 0.0).astype(jnp.float32) * (e_in if n else e_out)[n, r]
         energy_ref[j] = tile
 
-    for n in walk_ids:
-        tag_copies[n].wait_send()
-        slot_copies[n].wait_send()
-    links.finish()
+    store_grad.wait()
+
+
+def finish(parts_ref, grad_ref, energy_ref, out_ref):
+    out_ref[...] = grad_ref[...]
+
+    @pl.when(pl.program_id(0) == 0)
+    def _():
+        lanes = lax.broadcasted_iota(jnp.int32, energy_ref.shape, 1)
+        row = jnp.zeros(energy_ref.shape, jnp.float32)
+        for j in range(parts_ref.shape[0]):
+            row = jnp.where(lanes == j, jnp.sum(parts_ref[j]), row)
+        energy_ref[...] = row
 
 
 def body(orbitals, cholesky, parents, counts, steps):
@@ -395,7 +434,7 @@
             jax.ShapeDtypeStruct((per_device, electrons, basis), f32),
         ),
         in_specs=[pl.BlockSpec(memory_space=pltpu.SMEM)] * 2 + [pl.BlockSpec(memory_space=pl.ANY)] * 3,
-        out_specs=(pl.BlockSpec(memory_space=pltpu.VMEM), pl.BlockSpec(memory_space=pltpu.VMEM)),
+        out_specs=(pl.BlockSpec(memory_space=pltpu.VMEM), pl.BlockSpec(memory_space=pl.ANY)),
         scratch_shapes=[
             pltpu.VMEM((len(ORDER), vectors, electrons, basis), bf16),
             pltpu.VMEM((per_device, electrons, basis), bf16),
@@ -406,8 +445,9 @@
             pltpu.VMEM((reach, CAP, per_device, 128), f32),
             pltpu.VMEM((2, basis, half), bf16),
             pltpu.VMEM((2, half, basis), f32),
-            pltpu.VMEM((half, vectors * electrons), bf16),
+            pltpu.VMEM((2, half, vectors * electrons), bf16),
             pltpu.VMEM((reach * CAP, per_device, 8, 128), f32),
+            pltpu.VMEM((per_device, electrons, basis), f32),
             pltpu.VMEM((reach, CAP, 8, 128), f32),
             pltpu.VMEM((reach, CAP, 8, 128), f32),
             dma((3,)),
@@ -420,7 +460,17 @@
         ),
         name="exchange",
     )(parents.reshape(1, -1), counts, orbitals, cholesky, steps)
-    return jnp.sum(energy, axis=(1, 2)), grad
+    part = per_device // 4
+    grad_spec = pl.BlockSpec((part, electrons, basis), lambda i: (i, 0, 0))
+    energy, grad = pl.pallas_call(
+        finish,
+        grid=(4,),
+        out_shape=(jax.ShapeDtypeStruct((1, per_device), f32), jax.ShapeDtypeStruct(grad.shape, f32)),
+        in_specs=[pl.BlockSpec((per_device, 8, 128), lambda i: (0, 0, 0)), grad_spec],
+        out_specs=(pl.BlockSpec((1, per_device), lambda i: (0, 0)), grad_spec),
+        name="finish",
+    )(energy, grad)
+    return energy.reshape(per_device), grad
 
 
 def solution(mesh):

time: 110 us -> 108 us (0.982)
  local copies, waits for them, and re-layouts: 3.16 us -> 0 us
  Pallas kernels: 104 us -> 106 us
  other arithmetic: 1.41 us -> 0 us
    pallas_call x0 -> x1, Pallas kernels: none -> 3.92 us  [body(): pl.pallas_call(finish, grid=(4,), out_shape=(jax.ShapeDtypeStruct((1, per...]
    unnamed x1 -> x0, local copies, waits for them, and re-layouts: 3.16 us -> none
    pallas_call x1, Pallas kernels: 104 us -> 102 us  [body(): pl.pallas_call(kernel, out_shape=(jax.ShapeDtypeStruct((per_device, 8, 12...]
    reduce_sum x1 -> x0, other arithmetic: 1.41 us -> none  [body(): return (jnp.sum(energy, axis=(1, 2)), grad)]
where the time goes in v3:
time: 108 us
  Pallas kernels  106 us (98%)
  between operations  1.29 us (1%)
    pallas_call x1, Pallas kernels, body(): pl.pallas_call(kernel, out_shape=(jax.ShapeDtypeStruct((per_device, 8, 12...  102 us
    pallas_call x1, Pallas kernels, body(): pl.pallas_call(finish, grid=(4,), out_shape=(jax.ShapeDtypeStruct((1, per...  3.92 us

profile of v3, /device:TPU:1, one launch (start us, length us, event | category | flops | bytes accessed | tf_op | source)
XLA Modules:
  0.0 107.6 jit_solution(14067510617733756261)
XLA Ops:
  1.3 102.4 %exchange.1 = (f32[8,8,128]{2,1,0:T(8,128)}, f32[8,64,1024]{2,1,0:T(8,128)}) custom-call(s32[1,8]{1,0:T(1,128)} %bitcast.2, s32[1,1]{1,0:T(1,128)S(6)} %copy.7.counts, bf16[8,64,1024]{2,1,0:T(8,128)(2,1)} %orbitals_hbm.1, bf16[12,64,1024]{2,1,0:T(8,128)(2,1)} %cholesky_hbm.1, bf16[8,64,1024]{2,1,0:T(8,128)(2,1)} %steps_hbm.1), custom_call_target="tpu_custom_call" | custom-call | tf_op jit(solution)/shard_map/exchange/pallas_call | solution.py:430
  103.6 3.9 %finish.1 = (f32[1,8]{1,0:T(1,128)}, f32[8,64,1024]{2,1,0:T(8,128)}) custom-call(f32[8,8,128]{2,1,0:T(8,128)} %get-tuple-element.6.parts_ref, f32[8,64,1024]{2,1,0:T(8,128)} %get-tuple-element.7.grad_ref), custom_call_target="tpu_custom_call" | custom-call | tf_op jit(solution)/shard_map/finish/pallas_call | solution.py:465

commit v4 on v3

--- a/solution.py
+++ b/solution.py
@@ -254,7 +254,7 @@
         (15, x_arrived, (1, 1)),
         (16, far_arrived, (1,)),
         (17, far_turned, (0,)),
-        (19, x_arrived, (1, 0)),
+        (18, x_arrived, (1, 0)),
         (20, x_arrived, (1, 2)),
         (22, far_turned, (1,)),
         (23, x_arrived, (1, 3)),
@@ -413,11 +413,11 @@
 
     @pl.when(pl.program_id(0) == 0)
     def _():
-        lanes = lax.broadcasted_iota(jnp.int32, energy_ref.shape, 1)
-        row = jnp.zeros(energy_ref.shape, jnp.float32)
-        for j in range(parts_ref.shape[0]):
-            row = jnp.where(lanes == j, jnp.sum(parts_ref[j]), row)
-        energy_ref[...] = row
+        tile = jnp.sum(parts_ref[...], axis=1)
+        each = jnp.broadcast_to(jnp.sum(tile, axis=1, keepdims=True), tile.shape)
+        diagonal = lax.broadcasted_iota(jnp.int32, tile.shape, 0) == lax.broadcasted_iota(jnp.int32, tile.shape, 1)
+        row = jnp.sum(jnp.where(diagonal, each, 0.0), axis=0, keepdims=True)
+        energy_ref[...] = row[:, : energy_ref.shape[1]]
 
 
 def body(orbitals, cholesky, parents, counts, steps):
@@ -460,11 +460,11 @@
         ),
         name="exchange",
     )(parents.reshape(1, -1), counts, orbitals, cholesky, steps)
-    part = per_device // 4
+    part = per_device // 2
     grad_spec = pl.BlockSpec((part, electrons, basis), lambda i: (i, 0, 0))
     energy, grad = pl.pallas_call(
         finish,
-        grid=(4,),
+        grid=(2,),
         out_shape=(jax.ShapeDtypeStruct((1, per_device), f32), jax.ShapeDtypeStruct(grad.shape, f32)),
         in_specs=[pl.BlockSpec((per_device, 8, 128), lambda i: (0, 0, 0)), grad_spec],
         out_specs=(pl.BlockSpec((1, per_device), lambda i: (0, 0)), grad_spec),

time: 108 us -> 106 us (0.981)
    pallas_call x1, Pallas kernels: 3.92 us -> 2.72 us  [body(): pl.pallas_call(finish, grid=(2,), out_shape=(jax.ShapeDtypeStruct((1, per...]
where the time goes in v4:
time: 106 us
  Pallas kernels  105 us (99%)
  between operations  1.29 us (1%)
    pallas_call x1, Pallas kernels, body(): pl.pallas_call(kernel, out_shape=(jax.ShapeDtypeStruct((per_device, 8, 12...  102 us
    pallas_call x1, Pallas kernels, body(): pl.pallas_call(finish, grid=(2,), out_shape=(jax.ShapeDtypeStruct((1, per...  2.72 us

profile of v4, /device:TPU:1, one launch (start us, length us, event | category | flops | bytes accessed | tf_op | source)
XLA Modules:
  0.0 106.0 jit_solution(7512670995762687260)
XLA Ops:
  1.3 102.0 %exchange.1 = (f32[8,8,128]{2,1,0:T(8,128)}, f32[8,64,1024]{2,1,0:T(8,128)}) custom-call(s32[1,8]{1,0:T(1,128)} %bitcast.2, s32[1,1]{1,0:T(1,128)S(6)} %copy.7.counts, bf16[8,64,1024]{2,1,0:T(8,128)(2,1)} %orbitals_hbm.1, bf16[12,64,1024]{2,1,0:T(8,128)(2,1)} %cholesky_hbm.1, bf16[8,64,1024]{2,1,0:T(8,128)(2,1)} %steps_hbm.1), custom_call_target="tpu_custom_call" | custom-call | tf_op jit(solution)/shard_map/exchange/pallas_call | solution.py:430
  103.3 2.7 %finish.1 = (f32[1,8]{1,0:T(1,128)}, f32[8,64,1024]{2,1,0:T(8,128)}) custom-call(f32[8,8,128]{2,1,0:T(8,128)} %get-tuple-element.6.parts_ref, f32[8,64,1024]{2,1,0:T(8,128)} %get-tuple-element.7.grad_ref), custom_call_target="tpu_custom_call" | custom-call | tf_op jit(solution)/shard_map/finish/pallas_call | solution.py:465
